TPU v7x, 256 devices: a whole 4x4x8 slice. The times are simulated.
256 devices in a mesh: sub: 64 (over x, z, core), tile: 4 (over y).
Axes of the slice: x: 4, y: 4, z: 8, core: 2. Of those that a mesh axis runs over, the one named last changes fastest.
Arguments:
- coupling: bfloat16 [64, 28, 256, 256], P('sub'), may hold values from -0.125 to 0.125
- panel_inv: float32 [64, 8, 256, 256], P('sub')
- a_ib: bfloat16 [64, 2048, 3072], P('sub', None, 'tile'), may hold values from -0.5 to 0.5
- owner: int32 [64, 12, 12], P('sub', None, 'tile'), may hold values from 0 to 63, as said below
- slot: int32 [64, 12, 12], P('sub', None, 'tile'), may hold values from 0 to 15
- base: bfloat16 [64, 64, 256, 256], P('sub', 'tile'), may hold values from -2 to 2
Outputs:
- assembled: bfloat16 [64, 64, 256, 256], P('sub', 'tile')
Inputs may be any that keep to these rules, and one draw needn't show every extreme that they name: `owner`: tiles of one device are those of one subdomain s and tile columns t*12/4 to (t+1)*12/4 - 1. At most 1 tiles of one device name one sub index; for each t one sub index, drawn from the seed, is named by exactly 1 tiles of every device of that t.
All inputs are finite; a program needn't handle non-finite values.
Results may differ from a plain program's by a relative error of at most 0.0051.
Values may be sent and summed in bfloat16 or wider, within the bound.
No kernel may reach another device: no remote copies, remote signals or barrier semaphores. Data moves between devices by JAX's collectives and lax.ppermute only.
A program may use at most 128 MiB of HBM per device.

v0:
```python
import functools

import jax
import jax.numpy as jnp
from jax import lax
from jax.experimental import pallas as pl
from jax.experimental.pallas import tpu as pltpu
from jax.sharding import Mesh
from jax.sharding import PartitionSpec as P


SUB = ("sub_0", "sub_1", "sub_2")
NT = (((1,), (1,)), ((), ()))
CHUNKS = (16, 48, 96, 96)


def offsets():
    found, total = [], 0
    for rows in CHUNKS:
        found.append(total)
        total += rows
    return found


def solve_kernel(lower_ref, inverse_ref, right_ref, whole_ref, *rest):
    chunk_refs, joined_ref = rest[:-1], rest[-1]
    panels, panel = inverse_ref.shape[0], inverse_ref.shape[1]
    col_tiles = whole_ref.shape[0] // panel
    for k in range(panels):
        target = right_ref[k * panel : (k + 1) * panel, :].astype(jnp.float32).T
        if k > 0:
            first = k * (k - 1) // 2
            for m in range(k):
                joined_ref[:, m * panel : (m + 1) * panel] = lower_ref[first + m]
            target = target - lax.dot_general(
                whole_ref[:, : k * panel],
                joined_ref[:, : k * panel],
                NT,
                preferred_element_type=jnp.float32,
            )
        high = target.astype(jnp.bfloat16)
        low = (target - high.astype(jnp.float32)).astype(jnp.bfloat16)
        inverse = inverse_ref[k]
        inverse_high = inverse.astype(jnp.bfloat16)
        inverse_low = (inverse - inverse_high.astype(jnp.float32)).astype(jnp.bfloat16)
        product = functools.partial(
            lax.dot_general, dimension_numbers=NT, preferred_element_type=jnp.float32
        )
        solved = product(high, inverse_high) + (
            product(low, inverse_high) + product(high, inverse_low)
        )
        whole_ref[:, k * panel : (k + 1) * panel] = solved.astype(jnp.bfloat16)
    for ref, start, rows in zip(chunk_refs, offsets(), CHUNKS):
        for j in range(col_tiles):
            ref[j] = whole_ref[j * panel + start : j * panel + start + rows, :]


def solve(lower_blocks, inverse, right_cols):
    panel = inverse.shape[1]
    inner, cols = right_cols.shape
    col_tiles = cols // panel
    vmem = pl.BlockSpec(memory_space=pltpu.VMEM)
    return pl.pallas_call(
        solve_kernel,
        out_shape=[jax.ShapeDtypeStruct((cols, inner), jnp.bfloat16)]
        + [jax.ShapeDtypeStruct((col_tiles, rows, inner), jnp.bfloat16) for rows in CHUNKS],
        in_specs=[vmem] * 3,
        out_specs=[vmem] * (1 + len(CHUNKS)),
        scratch_shapes=[pltpu.VMEM((panel, inner - panel), jnp.bfloat16)],
        compiler_params=pltpu.CompilerParams(vmem_limit_bytes=40 * 1024 * 1024),
        cost_estimate=pl.CostEstimate(
            flops=12_000_000_000, bytes_accessed=16_000_000, transcendentals=0
        ),
        name="solve",
    )(lower_blocks, inverse, right_cols)


def gram_kernel(place_ref, owner_ref, own_ref, next_ref, far_ref, last_ref, whole_ref, seats_ref, left_ref):
    col_tiles, rows, _ = own_ref.shape
    panel = whole_ref.shape[0] // col_tiles
    groups = (own_ref, next_ref, far_ref, last_ref)
    for step, ref in enumerate(groups):
        for j in range(col_tiles):
            first = (step * col_tiles + j) * rows
            left_ref[first : first + rows, :] = ref[j]
    place = place_ref[0]

    def column(b, carry):
        right = whole_ref[pl.ds(pl.multiple_of(b * panel, panel), panel), :]
        block = lax.dot_general(left_ref[...], right, NT, preferred_element_type=jnp.float32)
        block = (-block).astype(jnp.bfloat16)
        for step in range(len(groups)):
            group = lax.rem(place + step, len(groups))
            for j in range(col_tiles):
                seat = owner_ref[(group * col_tiles + j) * col_tiles + b]
                first = (step * col_tiles + j) * rows
                seats_ref[seat] = block[first : first + rows, :]
        return carry

    lax.fori_loop(0, col_tiles, column, 0)


def gram(place, owners, parts, whole, peers):
    col_tiles, rows, inner = parts[0].shape
    cols = whole.shape[0]
    panel = cols // col_tiles
    vmem = pl.BlockSpec(memory_space=pltpu.VMEM)
    smem = pl.BlockSpec(memory_space=pltpu.SMEM)
    total = len(parts) * col_tiles * rows
    return pl.pallas_call(
        gram_kernel,
        out_shape=jax.ShapeDtypeStruct((peers, rows, panel), jnp.bfloat16),
        in_specs=[smem, smem] + [vmem] * 5,
        out_specs=vmem,
        scratch_shapes=[pltpu.VMEM((total, inner), jnp.bfloat16)],
        compiler_params=pltpu.CompilerParams(vmem_limit_bytes=32 * 1024 * 1024),
        cost_estimate=pl.CostEstimate(
            flops=2 * total * cols * inner,
            bytes_accessed=2 * (total * inner + cols * inner + peers * rows * panel),
            transcendentals=0,
        ),
        name="gram",
    )(place, owners, *parts, whole)


def row_block(start, rows):
    block = 32
    while start % block or rows % block:
        block //= 2
    return block


def collect_kernel(label_ref, seats_ref, base_ref, *refs):
    out_ref, total_ref = refs[-2:]
    total_ref[...] = base_ref[...].astype(jnp.float32)

    def one(p, carry):
        label = label_ref[p]

        @pl.when(label >= 0)
        def _():
            total_ref[label] = total_ref[label] + seats_ref[p].astype(jnp.float32)

        return carry

    lax.fori_loop(0, seats_ref.shape[0], one, 0, unroll=4)
    out_ref[...] = total_ref[...].astype(jnp.bfloat16)


def collect(labels, seats, base, current, start):
    peers, rows, panel = seats.shape
    slots = base.shape[0]
    block = row_block(start, rows)
    shift = start // block
    here = pl.BlockSpec((slots, block, panel), lambda i, _: (0, i + shift, 0))
    before = [] if current is None else [current]
    return pl.pallas_call(
        collect_kernel,
        out_shape=jax.ShapeDtypeStruct(base.shape, base.dtype),
        grid_spec=pltpu.PrefetchScalarGridSpec(
            num_scalar_prefetch=1,
            grid=(rows // block,),
            in_specs=[pl.BlockSpec((peers, block, panel), lambda i, _: (0, i, 0)), here]
            + [pl.BlockSpec(memory_space=pl.ANY)] * len(before),
            out_specs=here,
            scratch_shapes=[pltpu.VMEM((slots, block, panel), jnp.float32)],
        ),
        input_output_aliases={3: 0} if before else {},
        compiler_params=pltpu.CompilerParams(vmem_limit_bytes=16 * 1024 * 1024),
        cost_estimate=pl.CostEstimate(
            flops=2 * peers * rows * panel,
            bytes_accessed=2 * (peers + 2 * slots) * rows * panel,
            transcendentals=0,
        ),
        name="collect",
    )(labels, seats, base, *before)


def ring(length, step):
    return [(i, (i + step) % length) for i in range(length)]


def send(array, axis, step):
    return lax.ppermute(array, axis, ring(lax.axis_size(axis), step))


def trade(array, axes):
    return lax.all_to_all(array, axes, split_axis=0, concat_axis=0, tiled=True)


def shards(coupling, panel_inv, a_ib, owner, slot, base):
    return assemble(coupling[0], panel_inv[0], a_ib[0], owner[0], slot[0], base[0])[None]


def assemble(lower_blocks, inverse, right_cols, owner, slot, base):
    peers = lax.axis_size(SUB)
    owners = owner.reshape(-1)
    slots = slot.reshape(-1)
    position = jnp.arange(peers, dtype=jnp.int32)
    selected = position[:, None] == owners[None, :]
    labels = jnp.sum(jnp.where(selected, slots[None, :] + 1, 0), axis=1) - 1
    labels = trade(labels, SUB)
    place = lax.axis_index("tile").astype(jnp.int32).reshape(1)
    whole, *own = solve(lower_blocks, inverse, right_cols)
    current = None
    for i, start in enumerate(offsets()):
        part = own[i]
        below = send(part, "tile", 1)
        above = send(part, "tile", -1)
        far = send(*((below, "tile", 1) if i % 2 == 0 else (above, "tile", -1)))
        seats = gram(place, owners, (part, above, far, below), whole, peers)
        seats = trade(seats, SUB)
        current = collect(labels, seats, base, current, start)
    return current


def solution(mesh):
    torus = Mesh(
        mesh.devices.reshape(4, 8, 2, mesh.shape["tile"]), ("sub_0", "sub_1", "sub_2", "tile")
    )
    placed = (
        P(SUB, None, None, None),
        P(SUB, None, None, None),
        P(SUB, None, "tile"),
        P(SUB, None, "tile"),
        P(SUB, None, "tile"),
        P(SUB, "tile", None, None),
    )
    return jax.shard_map(
        shards, mesh=torus, in_specs=placed, out_specs=P(SUB, "tile", None, None), check_vma=False
    )
```

profile of v0, /device:TPU:33, one launch (start us, length us, event | category | flops | bytes accessed | tf_op | source)
XLA Modules:
  0.0 318.6 jit_solution(8778919272121434365)
XLA Ops:
  0.0 1.9 copy-done.5
  1.9 1.6 copy-done.6
  3.5 11.0 %solve.1 = (bf16[768,2048]{1,0:T(8,128)(2,1)S(1)}, bf16[3,16,2048]{2,1,0:T(8,128)(2,1)S(1)}, bf16[3,48,2048]{2,1,0:T(8,128)(2,1)}, bf16[3,96,2048]{2,1,0:T(8,128)(2,1)S(1)}, bf16[3,96,2048]{2,1,0:T(8,128)(2,1)S(1)}) custom-call(bf16[28,256,256]{2,1,0:T(8,128)(2,1)} %bitcast.14, f32[8,256,256]{2,1,0:T(8,128)S(1)} %bitcast.13, bf16[2048,768]{1,0:T(8,128)(2,1)S(1)} %bitcast.12), custom_call_target="tpu_custom_call" | custom-call | flops 12000000000 | bytes 16000000 | tf_op jit(solution)/shard_map/solve/pallas_call | solution.py:63
  14.5 1.0 copy-done.7
  15.5 1.0 copy-done.9
  16.6 1.3 collective-permute-start.10
  17.8 1.4 collective-permute-start.9
  19.3 1.5 collective-permute-start.6
  20.8 0.1 copy.20
  20.9 0.1 copy.21
  21.1 0.1 select_reduce_fusion
  21.2 2.4 collective-permute-done.10.last_ref
  23.7 0.7 copy.22
  24.5 13.1 %all-to-all-start = ((s32[64,1,1]{2,1,0:T(1,128)}), s32[64,1,1]{2,1,0:T(1,128)}, u32[]{:S(2)}, u32[]{:S(2)}) async-start(s32[64,1,1]{2,1,0:T(1,128)} %copy.22), calls=%async_computation | async-start | bytes 65536 | tf_op jit(solution)/shard_map/all_to_all | solution.py:188
  37.6 2.6 gram.7
  40.2 0.8 copy-done.4
  41.0 4.8 %all-to-all-done = s32[64,1,1]{2,1,0:T(1,128)} async-done(((s32[64,1,1]{2,1,0:T(1,128)}), s32[64,1,1]{2,1,0:T(1,128)}, u32[]{:S(2)}, u32[]{:S(2)}) %all-to-all-start) | async-done | bytes 288 | tf_op jit(solution)/shard_map/all_to_all | solution.py:188
  45.8 6.5 %all-to-all-start.4 = ((bf16[64,16,256]{2,1,0:T(8,128)(2,1)}), bf16[64,16,256]{2,1,0:T(8,128)(2,1)}, u32[]{:S(2)}, u32[]{:S(2)}) async-start(bf16[64,16,256]{2,1,0:T(8,128)(2,1)} %copy-done.4), calls=%async_computation.4 | async-start | bytes 1048576 | tf_op jit(solution)/shard_map/all_to_all | solution.py:188
  52.3 1.6 collective-permute-start.8
  53.9 1.5 collective-permute-start.7
  55.3 13.3 %collective-permute-done.8.last_ref = bf16[3,48,2048]{2,1,0:T(8,128)(2,1)S(1)} collective-permute-done((bf16[3,48,2048]{2,1,0:T(8,128)(2,1)}, bf16[3,48,2048]{2,1,0:T(8,128)(2,1)S(1)}, u32[]{:S(2)}, u32[]{:S(2)}) %collective-permute-start.8) | collective-permute-done | bytes 589856 | tf_op jit(solution)/shard_map/ppermute | solution.py:184
  68.6 3.8 %gram.6 = bf16[64,48,256]{2,1,0:T(8,128)(2,1)S(1)} custom-call(s32[1]{0:T(128)} %bitcast.1.place_ref, s32[36]{0:T(128)S(1)} %eq.16.owner_ref, bf16[3,48,2048]{2,1,0:T(8,128)(2,1)} %get-tuple-element.13.own_ref, bf16[3,48,2048]{2,1,0:T(8,128)(2,1)} %collective-permute-done.6.next_ref, bf16[3,48,2048]{2,1,0:T(8,128)(2,1)S(1)} %collective-permute-done.7.far_ref, ...), custom_call_target="tpu_custom_call" | custom-call | flops 1811939328 | bytes 7077888 | tf_op jit(solution)/shard_map/gram/pallas_call | solution.py:110
  72.5 1.1 copy-done.1
  73.6 11.4 %all-to-all-start.3 = ((bf16[64,48,256]{2,1,0:T(8,128)(2,1)}), bf16[64,48,256]{2,1,0:T(8,128)(2,1)}, u32[]{:S(2)}, u32[]{:S(2)}) async-start(bf16[64,48,256]{2,1,0:T(8,128)(2,1)} %copy-done.1), calls=%async_computation.3 | async-start | bytes 3145728 | tf_op jit(solution)/shard_map/all_to_all | solution.py:188
  85.0 1.1 collective-permute-start.4
  86.1 1.7 collective-permute-start.3
  87.9 25.9 %collective-permute-done.4.last_ref = bf16[3,96,2048]{2,1,0:T(8,128)(2,1)S(1)} collective-permute-done((bf16[3,96,2048]{2,1,0:T(8,128)(2,1)}, bf16[3,96,2048]{2,1,0:T(8,128)(2,1)S(1)}, u32[]{:S(2)}, u32[]{:S(2)}) %collective-permute-start.4) | collective-permute-done | bytes 1179680 | tf_op jit(solution)/shard_map/ppermute | solution.py:184
  113.8 27.6 %collective-permute-done.5.far_ref = bf16[3,96,2048]{2,1,0:T(8,128)(2,1)S(1)} collective-permute-done((bf16[3,96,2048]{2,1,0:T(8,128)(2,1)S(1)}, bf16[3,96,2048]{2,1,0:T(8,128)(2,1)S(1)}, u32[]{:S(2)}, u32[]{:S(2)}) %collective-permute-start.5) | collective-permute-done | bytes 1179680 | tf_op jit(solution)/shard_map/ppermute | solution.py:184
  141.4 1.3 copy-done.10
  142.6 5.1 %gram.5 = bf16[64,96,256]{2,1,0:T(8,128)(2,1)S(1)} custom-call(s32[1]{0:T(128)} %bitcast.1.place_ref, s32[36]{0:T(128)S(1)} %eq.16.owner_ref, bf16[3,96,2048]{2,1,0:T(8,128)(2,1)S(1)} %copy-done.10, bf16[3,96,2048]{2,1,0:T(8,128)(2,1)S(1)} %collective-permute-done.3.next_ref, bf16[3,96,2048]{2,1,0:T(8,128)(2,1)S(1)} %collective-permute-done.5.far_ref, ...), custom_call_target="tpu_custom_call" | custom-call | flops 3623878656 | bytes 11010048 | tf_op jit(solution)/shard_map/gram/pallas_call | solution.py:110
  147.8 1.7 copy-done.2
  149.5 12.0 %all-to-all-start.2 = ((bf16[64,96,256]{2,1,0:T(8,128)(2,1)}), bf16[64,96,256]{2,1,0:T(8,128)(2,1)}, u32[]{:S(2)}, u32[]{:S(2)}) async-start(bf16[64,96,256]{2,1,0:T(8,128)(2,1)} %copy-done.2), calls=%async_computation.2 | async-start | bytes 6291456 | tf_op jit(solution)/shard_map/all_to_all | solution.py:188
  161.5 0.4 collective-permute-start
  161.9 1.1 collective-permute-start.2
  163.1 26.0 %collective-permute-done.next_ref = bf16[3,96,2048]{2,1,0:T(8,128)(2,1)S(1)} collective-permute-done((bf16[3,96,2048]{2,1,0:T(8,128)(2,1)}, bf16[3,96,2048]{2,1,0:T(8,128)(2,1)S(1)}, u32[]{:S(2)}, u32[]{:S(2)}) %collective-permute-start) | collective-permute-done | bytes 1179680 | tf_op jit(solution)/shard_map/ppermute | solution.py:184
  189.1 1.5 collective-permute-start.1
  190.6 25.0 %collective-permute-done.1.far_ref = bf16[3,96,2048]{2,1,0:T(8,128)(2,1)S(1)} collective-permute-done((bf16[3,96,2048]{2,1,0:T(8,128)(2,1)S(1)}, bf16[3,96,2048]{2,1,0:T(8,128)(2,1)S(1)}, u32[]{:S(2)}, u32[]{:S(2)}) %collective-permute-start.1) | collective-permute-done | bytes 1179680 | tf_op jit(solution)/shard_map/ppermute | solution.py:184
  215.5 1.3 copy-done.8
  216.8 5.1 %gram.4 = bf16[64,96,256]{2,1,0:T(8,128)(2,1)S(1)} custom-call(s32[1]{0:T(128)} %bitcast.1.place_ref, s32[36]{0:T(128)S(1)} %eq.16.owner_ref, bf16[3,96,2048]{2,1,0:T(8,128)(2,1)S(1)} %copy-done.8, bf16[3,96,2048]{2,1,0:T(8,128)(2,1)S(1)} %collective-permute-done.next_ref, bf16[3,96,2048]{2,1,0:T(8,128)(2,1)S(1)} %collective-permute-done.1.far_ref, ...), custom_call_target="tpu_custom_call" | custom-call | flops 3623878656 | bytes 11010048 | tf_op jit(solution)/shard_map/gram/pallas_call | solution.py:110
  222.0 1.7 copy-done.3
  223.6 10.2 %all-to-all-done.2.seats_ref = bf16[64,96,256]{2,1,0:T(8,128)(2,1)} async-done(((bf16[64,96,256]{2,1,0:T(8,128)(2,1)}), bf16[64,96,256]{2,1,0:T(8,128)(2,1)}, u32[]{:S(2)}, u32[]{:S(2)}) %all-to-all-start.2) | async-done | bytes 3145760 | tf_op jit(solution)/shard_map/all_to_all | solution.py:188
  233.9 7.0 %all-to-all-start.1 = ((bf16[64,96,256]{2,1,0:T(8,128)(2,1)}), bf16[64,96,256]{2,1,0:T(8,128)(2,1)}, u32[]{:S(2)}, u32[]{:S(2)}) async-start(bf16[64,96,256]{2,1,0:T(8,128)(2,1)} %copy-done.3), calls=%async_computation.1 | async-start | bytes 6291456 | tf_op jit(solution)/shard_map/all_to_all | solution.py:188
  240.8 2.0 reduce.label_ref
  242.8 3.0 collect.4.refs_0_
  245.8 4.8 %collect.5.refs_0_ = bf16[16,256,256]{2,1,0:T(8,128)(2,1)} custom-call(s32[64]{0:T(128)S(1)} %reduce.label_ref, bf16[64,48,256]{2,1,0:T(8,128)(2,1)} %all-to-all-done.3.seats_ref, bf16[16,256,256]{2,1,0:T(8,128)(2,1)S(1)} %bitcast.9, bf16[16,256,256]{2,1,0:T(8,128)(2,1)} %collect.4.refs_0_), custom_call_target="tpu_custom_call", output_to_operand_aliasing={{}: (3, {})} | custom-call | flops 1572864 | bytes 2359296 | tf_op jit(solution)/shard_map/collect/pallas_call | solution.py:157
  250.6 5.4 %collect.6.refs_0_ = bf16[16,256,256]{2,1,0:T(8,128)(2,1)} custom-call(s32[64]{0:T(128)S(1)} %reduce.label_ref, bf16[64,96,256]{2,1,0:T(8,128)(2,1)} %all-to-all-done.2.seats_ref, bf16[16,256,256]{2,1,0:T(8,128)(2,1)S(1)} %bitcast.10, bf16[16,256,256]{2,1,0:T(8,128)(2,1)} %collect.5.refs_0_), custom_call_target="tpu_custom_call", output_to_operand_aliasing={{}: (3, {})} | custom-call | flops 3145728 | bytes 4718592 | tf_op jit(solution)/shard_map/collect/pallas_call | solution.py:157
  256.0 57.2 %all-to-all-done.1.seats_ref = bf16[64,96,256]{2,1,0:T(8,128)(2,1)} async-done(((bf16[64,96,256]{2,1,0:T(8,128)(2,1)}), bf16[64,96,256]{2,1,0:T(8,128)(2,1)}, u32[]{:S(2)}, u32[]{:S(2)}) %all-to-all-start.1) | async-done | bytes 3145760 | tf_op jit(solution)/shard_map/all_to_all | solution.py:188
  313.2 5.4 %collect.7 = bf16[16,256,256]{2,1,0:T(8,128)(2,1)} custom-call(s32[64]{0:T(128)S(1)} %reduce.label_ref, bf16[64,96,256]{2,1,0:T(8,128)(2,1)} %all-to-all-done.1.seats_ref, bf16[16,256,256]{2,1,0:T(8,128)(2,1)S(1)} %bitcast.11, bf16[16,256,256]{2,1,0:T(8,128)(2,1)} %collect.6.refs_0_), custom_call_target="tpu_custom_call", output_to_operand_aliasing={{}: (3, {})} | custom-call | flops 3145728 | bytes 4718592 | tf_op jit(solution)/shard_map/collect/pallas_call | solution.py:157
  (30 shorter events, 0.3 us)
Async XLA Ops:
  0.0 1.9 copy-start.5
  1.9 1.6 copy-start.6
  3.5 17.3 %copy-start.12 = (s32[1,12,3]{1,0,2:T(1,128)S(1)}, s32[1,12,3]{1,0,2:T(1,128)}, u32[]{:S(2)}) copy-start(s32[1,12,3]{1,0,2:T(1,128)} %param.10) | copy-start | bytes 436
  3.5 17.3 %copy-start.11 = (s32[1,12,3]{1,0,2:T(1,128)S(1)}, s32[1,12,3]{1,0,2:T(1,128)}, u32[]{:S(2)}) copy-start(s32[1,12,3]{1,0,2:T(1,128)} %param.9) | copy-start | bytes 436
  14.5 1.0 copy-start.7
  15.5 1.0 copy-start.9
  16.6 7.1 %collective-permute-start.10 = (bf16[3,16,2048]{2,1,0:T(8,128)(2,1)S(1)}, bf16[3,16,2048]{2,1,0:T(8,128)(2,1)S(1)}, u32[]{:S(2)}, u32[]{:S(2)}) collective-permute-start(bf16[3,16,2048]{2,1,0:T(8,128)(2,1)S(1)} %get-tuple-element.14.own_ref), channel_id=1, source_target_pairs={{0,1},{1,2},{2,3},{3,0},{4,5},{5,6},{6,7},{7,4},{8,9},{9,10},{10,1... | collective-permute-start | bytes 589832 | tf_op jit(solution)/shard_map/ppermute | solution.py:184
  17.8 19.7 %collective-permute-start.9 = (bf16[3,16,2048]{2,1,0:T(8,128)(2,1)S(1)}, bf16[3,16,2048]{2,1,0:T(8,128)(2,1)}, u32[]{:S(2)}, u32[]{:S(2)}) collective-permute-start(bf16[3,16,2048]{2,1,0:T(8,128)(2,1)S(1)} %get-tuple-element.14.own_ref), channel_id=1, source_target_pairs={{0,3},{1,0},{2,1},{3,2},{4,7},{5,4},{6,5},{7,6},{8,11},{9,8},{10,9... | collective-permute-start | bytes 589832 | tf_op jit(solution)/shard_map/ppermute | solution.py:184
  19.3 34.6 %collective-permute-start.6 = (bf16[3,48,2048]{2,1,0:T(8,128)(2,1)}, bf16[3,48,2048]{2,1,0:T(8,128)(2,1)}, u32[]{:S(2)}, u32[]{:S(2)}) collective-permute-start(bf16[3,48,2048]{2,1,0:T(8,128)(2,1)} %get-tuple-element.13.own_ref), channel_id=1, source_target_pairs={{0,3},{1,0},{2,1},{3,2},{4,7},{5,4},{6,5},{7,6},{8,11},{9,8},{10,9... | collective-permute-start | bytes 1769480 | tf_op jit(solution)/shard_map/ppermute | solution.py:184
  23.7 13.9 %collective-permute-start.11 = (bf16[3,16,2048]{2,1,0:T(8,128)(2,1)S(1)}, bf16[3,16,2048]{2,1,0:T(8,128)(2,1)}, u32[]{:S(2)}, u32[]{:S(2)}) collective-permute-start(bf16[3,16,2048]{2,1,0:T(8,128)(2,1)S(1)} %collective-permute-done.10.last_ref), channel_id=1, source_target_pairs={{0,1},{1,2},{2,3},{3,0},{4,5},{5,6},{6,7},{7,4},{8,9},{9,10},{10,1... | collective-permute-start | bytes 589832 | tf_op jit(solution)/shard_map/ppermute | solution.py:184
  24.5 21.3 %all-to-all-start = ((s32[64,1,1]{2,1,0:T(1,128)}), s32[64,1,1]{2,1,0:T(1,128)}, u32[]{:S(2)}, u32[]{:S(2)}) async-start(s32[64,1,1]{2,1,0:T(1,128)} %copy.22), calls=%async_computation | async-start | bytes 65536 | tf_op jit(solution)/shard_map/all_to_all | solution.py:188
  40.2 0.8 copy-start.4
  45.8 27.8 %all-to-all-start.4 = ((bf16[64,16,256]{2,1,0:T(8,128)(2,1)}), bf16[64,16,256]{2,1,0:T(8,128)(2,1)}, u32[]{:S(2)}, u32[]{:S(2)}) async-start(bf16[64,16,256]{2,1,0:T(8,128)(2,1)} %copy-done.4), calls=%async_computation.4 | async-start | bytes 1048576 | tf_op jit(solution)/shard_map/all_to_all | solution.py:188
  52.3 16.3 %collective-permute-start.8 = (bf16[3,48,2048]{2,1,0:T(8,128)(2,1)}, bf16[3,48,2048]{2,1,0:T(8,128)(2,1)S(1)}, u32[]{:S(2)}, u32[]{:S(2)}) collective-permute-start(bf16[3,48,2048]{2,1,0:T(8,128)(2,1)} %get-tuple-element.13.own_ref), channel_id=1, source_target_pairs={{0,1},{1,2},{2,3},{3,0},{4,5},{5,6},{6,7},{7,4},{8,9},{9,10},{10,1... | collective-permute-start | bytes 1769480 | tf_op jit(solution)/shard_map/ppermute | solution.py:184
  53.9 14.7 %collective-permute-start.7 = (bf16[3,48,2048]{2,1,0:T(8,128)(2,1)}, bf16[3,48,2048]{2,1,0:T(8,128)(2,1)S(1)}, u32[]{:S(2)}, u32[]{:S(2)}) collective-permute-start(bf16[3,48,2048]{2,1,0:T(8,128)(2,1)} %collective-permute-done.6.next_ref), channel_id=1, source_target_pairs={{0,3},{1,0},{2,1},{3,2},{4,7},{5,4},{6,5},{7,6},{8,11},{9,8},{10,9... | collective-permute-start | bytes 1769480 | tf_op jit(solution)/shard_map/ppermute | solution.py:184
  72.5 1.1 copy-start.1
  73.6 75.9 %all-to-all-start.3 = ((bf16[64,48,256]{2,1,0:T(8,128)(2,1)}), bf16[64,48,256]{2,1,0:T(8,128)(2,1)}, u32[]{:S(2)}, u32[]{:S(2)}) async-start(bf16[64,48,256]{2,1,0:T(8,128)(2,1)} %copy-done.1), calls=%async_computation.3 | async-start | bytes 3145728 | tf_op jit(solution)/shard_map/all_to_all | solution.py:188
  85.0 28.7 %collective-permute-start.4 = (bf16[3,96,2048]{2,1,0:T(8,128)(2,1)}, bf16[3,96,2048]{2,1,0:T(8,128)(2,1)S(1)}, u32[]{:S(2)}, u32[]{:S(2)}) collective-permute-start(bf16[3,96,2048]{2,1,0:T(8,128)(2,1)} %copy-done.9), channel_id=1, source_target_pairs={{0,1},{1,2},{2,3},{3,0},{4,5},{5,6},{6,7},{7,4},{8,9},{9,10},{10,1... | collective-permute-start | bytes 3538952 | tf_op jit(solution)/shard_map/ppermute | solution.py:184
  86.1 27.7 %collective-permute-start.3 = (bf16[3,96,2048]{2,1,0:T(8,128)(2,1)}, bf16[3,96,2048]{2,1,0:T(8,128)(2,1)S(1)}, u32[]{:S(2)}, u32[]{:S(2)}) collective-permute-start(bf16[3,96,2048]{2,1,0:T(8,128)(2,1)} %copy-done.9), channel_id=1, source_target_pairs={{0,3},{1,0},{2,1},{3,2},{4,7},{5,4},{6,5},{7,6},{8,11},{9,8},{10,9... | collective-permute-start | bytes 3538952 | tf_op jit(solution)/shard_map/ppermute | solution.py:184
  113.8 27.6 %collective-permute-start.5 = (bf16[3,96,2048]{2,1,0:T(8,128)(2,1)S(1)}, bf16[3,96,2048]{2,1,0:T(8,128)(2,1)S(1)}, u32[]{:S(2)}, u32[]{:S(2)}) collective-permute-start(bf16[3,96,2048]{2,1,0:T(8,128)(2,1)S(1)} %collective-permute-done.4.last_ref), channel_id=1, source_target_pairs={{0,1},{1,2},{2,3},{3,0},{4,5},{5,6},{6,7},{7,4},{8,9},{9,10},{10,1... | collective-permute-start | bytes 3538952 | tf_op jit(solution)/shard_map/ppermute | solution.py:184
  141.4 1.3 copy-start.10
  147.8 1.7 copy-start.2
  149.5 84.4 %all-to-all-start.2 = ((bf16[64,96,256]{2,1,0:T(8,128)(2,1)}), bf16[64,96,256]{2,1,0:T(8,128)(2,1)}, u32[]{:S(2)}, u32[]{:S(2)}) async-start(bf16[64,96,256]{2,1,0:T(8,128)(2,1)} %copy-done.2), calls=%async_computation.2 | async-start | bytes 6291456 | tf_op jit(solution)/shard_map/all_to_all | solution.py:188
  161.5 27.5 %collective-permute-start = (bf16[3,96,2048]{2,1,0:T(8,128)(2,1)}, bf16[3,96,2048]{2,1,0:T(8,128)(2,1)S(1)}, u32[]{:S(2)}, u32[]{:S(2)}) collective-permute-start(bf16[3,96,2048]{2,1,0:T(8,128)(2,1)} %copy-done.7), channel_id=1, source_target_pairs={{0,3},{1,0},{2,1},{3,2},{4,7},{5,4},{6,5},{7,6},{8,11},{9,8},{10,9... | collective-permute-start | bytes 3538952 | tf_op jit(solution)/shard_map/ppermute | solution.py:184
  161.9 28.7 %collective-permute-start.2 = (bf16[3,96,2048]{2,1,0:T(8,128)(2,1)}, bf16[3,96,2048]{2,1,0:T(8,128)(2,1)S(1)}, u32[]{:S(2)}, u32[]{:S(2)}) collective-permute-start(bf16[3,96,2048]{2,1,0:T(8,128)(2,1)} %copy-done.7), channel_id=1, source_target_pairs={{0,1},{1,2},{2,3},{3,0},{4,5},{5,6},{6,7},{7,4},{8,9},{9,10},{10,1... | collective-permute-start | bytes 3538952 | tf_op jit(solution)/shard_map/ppermute | solution.py:184
  189.1 26.5 %collective-permute-start.1 = (bf16[3,96,2048]{2,1,0:T(8,128)(2,1)S(1)}, bf16[3,96,2048]{2,1,0:T(8,128)(2,1)S(1)}, u32[]{:S(2)}, u32[]{:S(2)}) collective-permute-start(bf16[3,96,2048]{2,1,0:T(8,128)(2,1)S(1)} %collective-permute-done.next_ref), channel_id=1, source_target_pairs={{0,3},{1,0},{2,1},{3,2},{4,7},{5,4},{6,5},{7,6},{8,11},{9,8},{10,9... | collective-permute-start | bytes 3538952 | tf_op jit(solution)/shard_map/ppermute | solution.py:184
  215.5 1.3 copy-start.8
  221.9 1.7 copy-start.3
  223.6 19.2 %copy-start = (bf16[1,16,256,256]{3,2,1,0:T(8,128)(2,1)S(1)}, bf16[1,16,256,256]{3,2,1,0:T(8,128)(2,1)}, u32[]{:S(2)}) copy-start(bf16[1,16,256,256]{3,2,1,0:T(8,128)(2,1)} %param.11) | copy-start | bytes 6291460
  233.9 79.3 %all-to-all-start.1 = ((bf16[64,96,256]{2,1,0:T(8,128)(2,1)}), bf16[64,96,256]{2,1,0:T(8,128)(2,1)}, u32[]{:S(2)}, u32[]{:S(2)}) async-start(bf16[64,96,256]{2,1,0:T(8,128)(2,1)} %copy-done.3), calls=%async_computation.1 | async-start | bytes 6291456 | tf_op jit(solution)/shard_map/all_to_all | solution.py:188
where the time goes:
time: 322 us; the launch traced here: 319 us
  waiting for transfers between devices  192 us (60%)
  starting transfers between devices  63.3 us (20%)
  Pallas kernels  46.3 us (14%)
  local copies, waits for them, and re-layouts  14.4 us (4%)
    ppermute x12, waiting for transfers between devices, send(): return lax.ppermute(array, axis, ring(lax.axis_size(axis), step))  120 us
    all_to_all x5, waiting for transfers between devices, trade(): return lax.all_to_all(array, axes, split_axis=0, concat_axis=0, tiled=True)  72.2 us
    all_to_all x5, starting transfers between devices, trade(): return lax.all_to_all(array, axes, split_axis=0, concat_axis=0, tiled=True)  50.1 us
    pallas_call x4, Pallas kernels, collect(): pl.pallas_call(collect_kernel, out_shape=jax.ShapeDtypeStruct(base.shape,...  18.5 us
    pallas_call x4, Pallas kernels, gram(): pl.pallas_call(gram_kernel, out_shape=jax.ShapeDtypeStruct((peers, rows,...  16.7 us
    unnamed x27, local copies, waits for them, and re-layouts  13.5 us
    ppermute x12, starting transfers between devices, send(): return lax.ppermute(array, axis, ring(lax.axis_size(axis), step))  13.2 us
    pallas_call x1, Pallas kernels, solve(): pl.pallas_call(solve_kernel, out_shape=[jax.ShapeDtypeStruct((cols, inner...  11 us
  transfers between devices with their start and end apart: 17, of which 9 were waited for; matrix products, arithmetic and copies ran while one was open for 1% of the time, Pallas kernels for 9%

commit v1 on v0

--- a/solution.py
+++ b/solution.py
@@ -11,7 +11,7 @@
 
 SUB = ("sub_0", "sub_1", "sub_2")
 NT = (((1,), (1,)), ((), ()))
-CHUNKS = (16, 48, 96, 96)
+CHUNKS = (32, 64, 96, 64)
 
 
 def offsets():
@@ -130,50 +130,62 @@
     return block
 
 
-def collect_kernel(label_ref, seats_ref, base_ref, *refs):
+def collect_kernel(core_ref, label_ref, own_ref, other_ref, base_ref, *refs):
     out_ref, total_ref = refs[-2:]
     total_ref[...] = base_ref[...].astype(jnp.float32)
+    chips = own_ref.shape[0]
+    cores = label_ref.shape[0] // chips
+    core = core_ref[0]
 
     def one(p, carry):
-        label = label_ref[p]
-
-        @pl.when(label >= 0)
+        own = label_ref[p * cores + core]
+        other = label_ref[p * cores + cores - 1 - core]
+
+        @pl.when(own >= 0)
         def _():
-            total_ref[label] = total_ref[label] + seats_ref[p].astype(jnp.float32)
+            total_ref[own] = total_ref[own] + own_ref[p, 0].astype(jnp.float32)
+
+        @pl.when(other >= 0)
+        def _():
+            total_ref[other] = total_ref[other] + other_ref[p].astype(jnp.float32)
 
         return carry
 
-    lax.fori_loop(0, seats_ref.shape[0], one, 0, unroll=4)
+    lax.fori_loop(0, chips, one, 0, unroll=2)
     out_ref[...] = total_ref[...].astype(jnp.bfloat16)
 
 
-def collect(labels, seats, base, current, start):
-    peers, rows, panel = seats.shape
+def collect(core, labels, arrived, other, base, current, start):
+    chips, _, rows, panel = arrived.shape
     slots = base.shape[0]
     block = row_block(start, rows)
     shift = start // block
-    here = pl.BlockSpec((slots, block, panel), lambda i, _: (0, i + shift, 0))
+    here = pl.BlockSpec((slots, block, panel), lambda i, *_: (0, i + shift, 0))
     before = [] if current is None else [current]
     return pl.pallas_call(
         collect_kernel,
         out_shape=jax.ShapeDtypeStruct(base.shape, base.dtype),
         grid_spec=pltpu.PrefetchScalarGridSpec(
-            num_scalar_prefetch=1,
+            num_scalar_prefetch=2,
             grid=(rows // block,),
-            in_specs=[pl.BlockSpec((peers, block, panel), lambda i, _: (0, i, 0)), here]
+            in_specs=[
+                pl.BlockSpec((chips, 1, block, panel), lambda i, *_: (0, 0, i, 0)),
+                pl.BlockSpec((chips, block, panel), lambda i, *_: (0, i, 0)),
+                here,
+            ]
             + [pl.BlockSpec(memory_space=pl.ANY)] * len(before),
             out_specs=here,
             scratch_shapes=[pltpu.VMEM((slots, block, panel), jnp.float32)],
         ),
-        input_output_aliases={3: 0} if before else {},
+        input_output_aliases={5: 0} if before else {},
         compiler_params=pltpu.CompilerParams(vmem_limit_bytes=16 * 1024 * 1024),
         cost_estimate=pl.CostEstimate(
-            flops=2 * peers * rows * panel,
-            bytes_accessed=2 * (peers + 2 * slots) * rows * panel,
+            flops=4 * chips * rows * panel,
+            bytes_accessed=4 * (chips + slots) * rows * panel,
             transcendentals=0,
         ),
         name="collect",
-    )(labels, seats, base, *before)
+    )(core, labels, arrived, other, base, *before)
 
 
 def ring(length, step):
@@ -201,16 +213,22 @@
     labels = jnp.sum(jnp.where(selected, slots[None, :] + 1, 0), axis=1) - 1
     labels = trade(labels, SUB)
     place = lax.axis_index("tile").astype(jnp.int32).reshape(1)
+    cores = lax.axis_size("sub_2")
+    core = lax.axis_index("sub_2").astype(jnp.int32)
+    seat_of = owners // cores * cores + (owners - core + cores) % cores
+    core = core.reshape(1)
     whole, *own = solve(lower_blocks, inverse, right_cols)
     current = None
     for i, start in enumerate(offsets()):
         part = own[i]
         below = send(part, "tile", 1)
         above = send(part, "tile", -1)
-        far = send(*((below, "tile", 1) if i % 2 == 0 else (above, "tile", -1)))
-        seats = gram(place, owners, (part, above, far, below), whole, peers)
-        seats = trade(seats, SUB)
-        current = collect(labels, seats, base, current, start)
+        far = send(part, "tile", 2)
+        seats = gram(place, seat_of, (part, above, far, below), whole, peers)
+        seats = seats.reshape(peers // cores, cores, part.shape[1], base.shape[1])
+        arrived = trade(seats, ("sub_0", "sub_1"))
+        other = send(arrived[:, 1], "sub_2", 1)
+        current = collect(core, labels, arrived, other, base, current, start)
     return current
 
 

time: 322 us -> 350 us (1.087)
  waiting for transfers between devices: 192 us -> 210 us
  blocking collectives: 0 us -> 13.4 us
  local copies, waits for them, and re-layouts: 14.4 us -> 26 us
  starting transfers between devices: 63.3 us -> 52.8 us
    ppermute x12 -> x16, waiting for transfers between devices: 120 us -> 142 us  [send(): return lax.ppermute(array, axis, ring(lax.axis_size(axis), step))]
    all_to_all x0 -> x1, blocking collectives: none -> 13.4 us  [trade(): return lax.all_to_all(array, axes, split_axis=0, concat_axis=0, tiled=True)]
    all_to_all x5 -> x4, starting transfers between devices: 50.1 us -> 36.9 us  [trade(): return lax.all_to_all(array, axes, split_axis=0, concat_axis=0, tiled=True)]
    squeeze x0 -> x4, local copies, waits for them, and re-layouts: none -> 6.58 us  [assemble(): other = send(arrived[:, 1], 'sub_2', 1)]
    unnamed x27 -> x45, local copies, waits for them, and re-layouts: 13.5 us -> 19.1 us
    all_to_all x5 -> x4, waiting for transfers between devices: 72.2 us -> 67.9 us  [trade(): return lax.all_to_all(array, axes, split_axis=0, concat_axis=0, tiled=True)]
    ppermute x12 -> x16, starting transfers between devices: 13.2 us -> 15.9 us  [send(): return lax.ppermute(array, axis, ring(lax.axis_size(axis), step))]
  transfers between devices with their start and end apart: 17 -> 20, of which waited for: 9 -> 14; matrix products, arithmetic and copies ran while one was open for 1% -> 2% of each run, Pallas kernels for 9% -> 7%
where the time goes in v1:
time: 350 us; the launch traced here: 347 us
  waiting for transfers between devices  210 us (60%)
  starting transfers between devices  52.8 us (15%)
  Pallas kernels  43.4 us (12%)
  local copies, waits for them, and re-layouts  26 us (7%)
  blocking collectives  13.4 us (4%)
    ppermute x16, waiting for transfers between devices, send(): return lax.ppermute(array, axis, ring(lax.axis_size(axis), step))  142 us
    all_to_all x4, waiting for transfers between devices, trade(): return lax.all_to_all(array, axes, split_axis=0, concat_axis=0, tiled=True)  67.9 us
    all_to_all x4, starting transfers between devices, trade(): return lax.all_to_all(array, axes, split_axis=0, concat_axis=0, tiled=True)  36.9 us
    unnamed x45, local copies, waits for them, and re-layouts  19.1 us
    pallas_call x4, Pallas kernels, gram(): pl.pallas_call(gram_kernel, out_shape=jax.ShapeDtypeStruct((peers, rows,...  16.5 us
    ppermute x16, starting transfers between devices, send(): return lax.ppermute(array, axis, ring(lax.axis_size(axis), step))  15.9 us
    pallas_call x4, Pallas kernels, collect(): pl.pallas_call(collect_kernel, out_shape=jax.ShapeDtypeStruct(base.shape,...  15.9 us
    all_to_all x1, blocking collectives, trade(): return lax.all_to_all(array, axes, split_axis=0, concat_axis=0, tiled=True)  13.4 us
  transfers between devices with their start and end apart: 20, of which 14 were waited for; matrix products, arithmetic and copies ran while one was open for 2% of the time, Pallas kernels for 7%

profile of v1, /device:TPU:33, one launch (start us, length us, event | category | flops | bytes accessed | tf_op | source)
XLA Modules:
  0.0 347.2 jit_solution(12594303395033581931)
XLA Ops:
  0.0 1.9 copy-done.14
  1.9 1.6 copy-done.15
  3.5 11.1 %solve.1 = (bf16[768,2048]{1,0:T(8,128)(2,1)S(1)}, bf16[3,32,2048]{2,1,0:T(8,128)(2,1)S(1)}, bf16[3,64,2048]{2,1,0:T(8,128)(2,1)}, bf16[3,96,2048]{2,1,0:T(8,128)(2,1)S(1)}, bf16[3,64,2048]{2,1,0:T(8,128)(2,1)S(1)}) custom-call(bf16[28,256,256]{2,1,0:T(8,128)(2,1)} %bitcast.39, f32[8,256,256]{2,1,0:T(8,128)S(1)} %bitcast.38, bf16[2048,768]{1,0:T(8,128)(2,1)S(1)} %bitcast.37), custom_call_target="tpu_custom_call" | custom-call | flops 12000000000 | bytes 16000000 | tf_op jit(solution)/shard_map/solve/pallas_call | solution.py:63
  16.5 1.3 collective-permute-start.10
  17.8 1.4 collective-permute-start.8
  19.2 1.6 collective-permute-start.9
  21.0 15.5 %collective-permute-done.10.last_ref = bf16[3,64,2048]{2,1,0:T(8,128)(2,1)} collective-permute-done((bf16[3,64,2048]{2,1,0:T(8,128)(2,1)}, bf16[3,64,2048]{2,1,0:T(8,128)(2,1)}, u32[]{:S(2)}, u32[]{:S(2)}) %collective-permute-start.10) | collective-permute-done | bytes 786464 | tf_op jit(solution)/shard_map/ppermute | solution.py:196
  36.5 18.0 %collective-permute-done.9.far_ref = bf16[3,64,2048]{2,1,0:T(8,128)(2,1)} collective-permute-done((bf16[3,64,2048]{2,1,0:T(8,128)(2,1)}, bf16[3,64,2048]{2,1,0:T(8,128)(2,1)}, u32[]{:S(2)}, u32[]{:S(2)}) %collective-permute-start.9) | collective-permute-done | bytes 786464 | tf_op jit(solution)/shard_map/ppermute | solution.py:196
  54.5 5.1 %gram.6 = bf16[64,64,256]{2,1,0:T(8,128)(2,1)S(1)} custom-call(s32[1]{0:T(128)} %bitcast.2.place_ref, s32[36]{0:T(128)S(1)} %fusion.owner_ref, bf16[3,64,2048]{2,1,0:T(8,128)(2,1)} %get-tuple-element.13.own_ref, bf16[3,64,2048]{2,1,0:T(8,128)(2,1)} %collective-permute-done.8.next_ref, bf16[3,64,2048]{2,1,0:T(8,128)(2,1)} %collective-permute-done.9.far_ref, ...), custom_call_target="tpu_custom_call" | custom-call | flops 2415919104 | bytes 8388608 | tf_op jit(solution)/shard_map/gram/pallas_call | solution.py:110
  59.6 1.3 copy-done.13
  61.0 10.8 %all-to-all-start.3 = ((bf16[32,2,64,256]{3,2,1,0:T(8,128)(2,1)}), bf16[32,2,64,256]{3,2,1,0:T(8,128)(2,1)S(1)}, u32[]{:S(2)}, u32[]{:S(2)}) async-start(bf16[32,2,64,256]{3,2,1,0:T(8,128)(2,1)} %bitcast.36), calls=%async_computation.3 | async-start | bytes 4194304 | tf_op jit(solution)/shard_map/all_to_all | solution.py:200
  72.8 1.4 collective-permute-start.1
  74.2 14.6 %collective-permute-done.next_ref = bf16[3,64,2048]{2,1,0:T(8,128)(2,1)S(1)} collective-permute-done((bf16[3,64,2048]{2,1,0:T(8,128)(2,1)S(1)}, bf16[3,64,2048]{2,1,0:T(8,128)(2,1)S(1)}, u32[]{:S(2)}, u32[]{:S(2)}) %collective-permute-start) | collective-permute-done | bytes 786464 | tf_op jit(solution)/shard_map/ppermute | solution.py:196
  88.8 1.8 collective-permute-done.1.far_ref
  90.7 20.0 %collective-permute-done.2.last_ref = bf16[3,64,2048]{2,1,0:T(8,128)(2,1)S(1)} collective-permute-done((bf16[3,64,2048]{2,1,0:T(8,128)(2,1)S(1)}, bf16[3,64,2048]{2,1,0:T(8,128)(2,1)S(1)}, u32[]{:S(2)}, u32[]{:S(2)}) %collective-permute-start.2) | collective-permute-done | bytes 786464 | tf_op jit(solution)/shard_map/ppermute | solution.py:196
  110.7 1.9 copy-done.8
  112.5 3.8 %gram.4 = bf16[64,64,256]{2,1,0:T(8,128)(2,1)S(1)} custom-call(s32[1]{0:T(128)} %bitcast.2.place_ref, s32[36]{0:T(128)S(1)} %fusion.owner_ref, bf16[3,64,2048]{2,1,0:T(8,128)(2,1)S(1)} %copy-done.19, bf16[3,64,2048]{2,1,0:T(8,128)(2,1)S(1)} %collective-permute-done.next_ref, bf16[3,64,2048]{2,1,0:T(8,128)(2,1)S(1)} %collective-permute-done.1.far_ref, ...), custom_call_target="tpu_custom_call" | custom-call | flops 2415919104 | bytes 8388608 | tf_op jit(solution)/shard_map/gram/pallas_call | solution.py:110
  116.3 1.3 copy-done.12
  117.7 3.3 all-to-all-done.3.own_ref
  121.0 1.4 copy-done.3
  122.4 6.5 %all-to-all-start.1 = ((bf16[32,2,64,256]{3,2,1,0:T(8,128)(2,1)}), bf16[32,2,64,256]{3,2,1,0:T(8,128)(2,1)}, u32[]{:S(2)}, u32[]{:S(2)}) async-start(bf16[32,2,64,256]{3,2,1,0:T(8,128)(2,1)} %bitcast.35), calls=%async_computation.1 | async-start | bytes 4194304 | tf_op jit(solution)/shard_map/all_to_all | solution.py:200
  129.6 1.6 collective-permute-start.5
  131.1 23.8 %collective-permute-done.4.next_ref = bf16[3,96,2048]{2,1,0:T(8,128)(2,1)S(1)} collective-permute-done((bf16[3,96,2048]{2,1,0:T(8,128)(2,1)}, bf16[3,96,2048]{2,1,0:T(8,128)(2,1)S(1)}, u32[]{:S(2)}, u32[]{:S(2)}) %collective-permute-start.4) | collective-permute-done | bytes 1179680 | tf_op jit(solution)/shard_map/ppermute | solution.py:196
  154.9 1.7 collective-permute-done.5.far_ref
  156.6 27.9 %collective-permute-done.6.last_ref = bf16[3,96,2048]{2,1,0:T(8,128)(2,1)S(1)} collective-permute-done((bf16[3,96,2048]{2,1,0:T(8,128)(2,1)}, bf16[3,96,2048]{2,1,0:T(8,128)(2,1)S(1)}, u32[]{:S(2)}, u32[]{:S(2)}) %collective-permute-start.6) | collective-permute-done | bytes 1179680 | tf_op jit(solution)/shard_map/ppermute | solution.py:196
  184.5 1.9 copy-done.9
  186.4 1.3 copy-done.17
  187.6 5.1 %gram.5 = bf16[64,96,256]{2,1,0:T(8,128)(2,1)S(1)} custom-call(s32[1]{0:T(128)} %bitcast.2.place_ref, s32[36]{0:T(128)S(1)} %fusion.owner_ref, bf16[3,96,2048]{2,1,0:T(8,128)(2,1)S(1)} %copy-done.17, bf16[3,96,2048]{2,1,0:T(8,128)(2,1)S(1)} %collective-permute-done.4.next_ref, bf16[3,96,2048]{2,1,0:T(8,128)(2,1)S(1)} %collective-permute-done.5.far_ref, ...), custom_call_target="tpu_custom_call" | custom-call | flops 3623878656 | bytes 11010048 | tf_op jit(solution)/shard_map/gram/pallas_call | solution.py:110
  192.8 1.7 copy-done.11
  194.5 9.2 %all-to-all-start.2 = ((bf16[32,2,96,256]{3,2,1,0:T(8,128)(2,1)}), bf16[32,2,96,256]{3,2,1,0:T(8,128)(2,1)S(1)}, u32[]{:S(2)}, u32[]{:S(2)}) async-start(bf16[32,2,96,256]{3,2,1,0:T(8,128)(2,1)} %bitcast.34), calls=%async_computation.2 | async-start | bytes 6291456 | tf_op jit(solution)/shard_map/all_to_all | solution.py:200
  203.8 1.4 collective-permute-start.13
  206.0 7.4 %collective-permute-done.12.next_ref = bf16[3,32,2048]{2,1,0:T(8,128)(2,1)S(1)} collective-permute-done((bf16[3,32,2048]{2,1,0:T(8,128)(2,1)S(1)}, bf16[3,32,2048]{2,1,0:T(8,128)(2,1)S(1)}, u32[]{:S(2)}, u32[]{:S(2)}) %collective-permute-start.12) | collective-permute-done | bytes 393248 | tf_op jit(solution)/shard_map/ppermute | solution.py:196
  214.5 10.3 %collective-permute-done.14.last_ref = bf16[3,32,2048]{2,1,0:T(8,128)(2,1)S(1)} collective-permute-done((bf16[3,32,2048]{2,1,0:T(8,128)(2,1)S(1)}, bf16[3,32,2048]{2,1,0:T(8,128)(2,1)S(1)}, u32[]{:S(2)}, u32[]{:S(2)}) %collective-permute-start.14) | collective-permute-done | bytes 393248 | tf_op jit(solution)/shard_map/ppermute | solution.py:196
  224.8 1.9 copy-done.10
  226.7 2.5 gram.7
  230.2 44.0 %all-to-all-done.2.own_ref = bf16[32,2,96,256]{3,2,1,0:T(8,128)(2,1)S(1)} async-done(((bf16[32,2,96,256]{3,2,1,0:T(8,128)(2,1)}), bf16[32,2,96,256]{3,2,1,0:T(8,128)(2,1)S(1)}, u32[]{:S(2)}, u32[]{:S(2)}) %all-to-all-start.2) | async-done | bytes 3145760 | tf_op jit(solution)/shard_map/all_to_all | solution.py:200
  274.1 10.4 %all-to-all-start.4 = ((bf16[32,2,32,256]{3,2,1,0:T(8,128)(2,1)}), bf16[32,2,32,256]{3,2,1,0:T(8,128)(2,1)}, u32[]{:S(2)}, u32[]{:S(2)}) async-start(bf16[32,2,32,256]{3,2,1,0:T(8,128)(2,1)} %bitcast.33), calls=%async_computation.4 | async-start | bytes 2097152 | tf_op jit(solution)/shard_map/all_to_all | solution.py:200
  284.6 1.3 slice_bitcast_fusion
  288.9 2.3 slice_bitcast_fusion.2
  291.3 20.6 %all-to-all-done.4.own_ref = bf16[32,2,32,256]{3,2,1,0:T(8,128)(2,1)} async-done(((bf16[32,2,32,256]{3,2,1,0:T(8,128)(2,1)}), bf16[32,2,32,256]{3,2,1,0:T(8,128)(2,1)}, u32[]{:S(2)}, u32[]{:S(2)}) %all-to-all-start.4) | async-done | bytes 1048608 | tf_op jit(solution)/shard_map/all_to_all | solution.py:200
  311.9 1.9 slice_bitcast_fusion.3
  313.8 2.4 collective-permute-start.15
  316.6 13.4 %all_to_all.28 = s32[64,1,1]{2,1,0:T(1,128)S(1)} all-to-all(s32[64,1,1]{2,1,0:T(1,128)S(1)} %copy.42), channel_id=1, replica_groups=mesh['sub_0'=4,'sub_1'=8,'sub_2'=2,'tile'=4] {'sub_0','sub_1','sub_2'}, dimensions={0} | all-to-all | bytes 512 | tf_op jit(solution)/shard_map/all_to_all | solution.py:200
  330.0 1.2 reduce.label_ref
  331.3 3.2 collect.4.refs_0_
  334.5 4.1 %collect.5.refs_0_ = bf16[16,256,256]{2,1,0:T(8,128)(2,1)} custom-call(s32[1]{0:T(128)} %bitcast.core_ref, s32[64]{0:T(128)S(1)} %reduce.label_ref, bf16[32,2,64,256]{3,2,1,0:T(8,128)(2,1)S(1)} %copy-done.5, bf16[32,64,256]{2,1,0:T(8,128)(2,1)} %collective-permute-done.11.other_ref, ...), custom_call_target="tpu_custom_call", output_to_operand_aliasing={{}: (5, {})} | custom-call | flops 2097152 | bytes 3145728 | tf_op jit(solution)/shard_map/collect/pallas_call | solution.py:165
  338.6 4.9 %collect.6.refs_0_ = bf16[16,256,256]{2,1,0:T(8,128)(2,1)} custom-call(s32[1]{0:T(128)} %bitcast.core_ref, s32[64]{0:T(128)S(1)} %reduce.label_ref, bf16[32,2,96,256]{3,2,1,0:T(8,128)(2,1)S(1)} %copy-done.2, bf16[32,96,256]{2,1,0:T(8,128)(2,1)} %collective-permute-done.7.other_ref, ...), custom_call_target="tpu_custom_call", output_to_operand_aliasing={{}: (5, {})} | custom-call | flops 3145728 | bytes 4718592 | tf_op jit(solution)/shard_map/collect/pallas_call | solution.py:165
  343.5 3.7 %collect.7 = bf16[16,256,256]{2,1,0:T(8,128)(2,1)} custom-call(s32[1]{0:T(128)} %bitcast.core_ref, s32[64]{0:T(128)S(1)} %reduce.label_ref, bf16[32,2,64,256]{3,2,1,0:T(8,128)(2,1)} %all-to-all-done.1.own_ref, bf16[32,64,256]{2,1,0:T(8,128)(2,1)S(1)} %collective-permute-done.3.other_ref, ...), custom_call_target="tpu_custom_call", output_to_operand_aliasing={{}: (5, {})} | custom-call | flops 2097152 | bytes 3145728 | tf_op jit(solution)/shard_map/collect/pallas_call | solution.py:165
  (60 shorter events, 10.5 us)
Async XLA Ops:
  0.0 1.9 copy-start.14
  1.9 1.6 copy-start.15
  3.5 17.4 %copy-start.20 = (s32[1,12,3]{1,0,2:T(1,128)S(1)}, s32[1,12,3]{1,0,2:T(1,128)}, u32[]{:S(2)}) copy-start(s32[1,12,3]{1,0,2:T(1,128)} %param.9) | copy-start | bytes 436
  14.6 1.0 copy-start.16
  15.6 0.9 copy-start.18
  16.5 43.1 %copy-start.7 = (bf16[768,2048]{1,0:T(8,128)(2,1)}, bf16[768,2048]{1,0:T(8,128)(2,1)S(1)}, u32[]{:S(2)}) copy-start(bf16[768,2048]{1,0:T(8,128)(2,1)S(1)} %get-tuple-element.11.whole_ref) | copy-start | bytes 9437188
  16.5 20.1 %collective-permute-start.10 = (bf16[3,64,2048]{2,1,0:T(8,128)(2,1)}, bf16[3,64,2048]{2,1,0:T(8,128)(2,1)}, u32[]{:S(2)}, u32[]{:S(2)}) collective-permute-start(bf16[3,64,2048]{2,1,0:T(8,128)(2,1)} %get-tuple-element.13.own_ref), channel_id=1, source_target_pairs={{0,1},{1,2},{2,3},{3,0},{4,5},{5,6},{6,7},{7,4},{8,9},{9,10},{10,1... | collective-permute-start | bytes 2359304 | tf_op jit(solution)/shard_map/ppermute | solution.py:196
  17.8 18.8 %collective-permute-start.8 = (bf16[3,64,2048]{2,1,0:T(8,128)(2,1)}, bf16[3,64,2048]{2,1,0:T(8,128)(2,1)}, u32[]{:S(2)}, u32[]{:S(2)}) collective-permute-start(bf16[3,64,2048]{2,1,0:T(8,128)(2,1)} %get-tuple-element.13.own_ref), channel_id=1, source_target_pairs={{0,3},{1,0},{2,1},{3,2},{4,7},{5,4},{6,5},{7,6},{8,11},{9,8},{10,9... | collective-permute-start | bytes 2359304 | tf_op jit(solution)/shard_map/ppermute | solution.py:196
  19.2 35.3 %collective-permute-start.9 = (bf16[3,64,2048]{2,1,0:T(8,128)(2,1)}, bf16[3,64,2048]{2,1,0:T(8,128)(2,1)}, u32[]{:S(2)}, u32[]{:S(2)}) collective-permute-start(bf16[3,64,2048]{2,1,0:T(8,128)(2,1)} %get-tuple-element.13.own_ref), channel_id=1, source_target_pairs={{0,2},{1,3},{2,0},{3,1},{4,6},{5,7},{6,4},{7,5},{8,10},{9,11},{10,... | collective-permute-start | bytes 2359304 | tf_op jit(solution)/shard_map/ppermute | solution.py:196
  59.6 1.3 copy-start.13
  61.0 10.8 %copy-start.19 = (bf16[3,64,2048]{2,1,0:T(8,128)(2,1)S(1)}, bf16[3,64,2048]{2,1,0:T(8,128)(2,1)}, u32[]{:S(2)}) copy-start(bf16[3,64,2048]{2,1,0:T(8,128)(2,1)} %copy-done.18) | copy-start | bytes 2359300
  61.0 60.0 %all-to-all-start.3 = ((bf16[32,2,64,256]{3,2,1,0:T(8,128)(2,1)}), bf16[32,2,64,256]{3,2,1,0:T(8,128)(2,1)S(1)}, u32[]{:S(2)}, u32[]{:S(2)}) async-start(bf16[32,2,64,256]{3,2,1,0:T(8,128)(2,1)} %bitcast.36), calls=%async_computation.3 | async-start | bytes 4194304 | tf_op jit(solution)/shard_map/all_to_all | solution.py:200
  71.7 17.1 %collective-permute-start = (bf16[3,64,2048]{2,1,0:T(8,128)(2,1)S(1)}, bf16[3,64,2048]{2,1,0:T(8,128)(2,1)S(1)}, u32[]{:S(2)}, u32[]{:S(2)}) collective-permute-start(bf16[3,64,2048]{2,1,0:T(8,128)(2,1)S(1)} %copy-done.19), channel_id=1, source_target_pairs={{0,3},{1,0},{2,1},{3,2},{4,7},{5,4},{6,5},{7,6},{8,11},{9,8},{10,9... | collective-permute-start | bytes 2359304 | tf_op jit(solution)/shard_map/ppermute | solution.py:196
  72.8 17.8 %collective-permute-start.1 = (bf16[3,64,2048]{2,1,0:T(8,128)(2,1)S(1)}, bf16[3,64,2048]{2,1,0:T(8,128)(2,1)S(1)}, u32[]{:S(2)}, u32[]{:S(2)}) collective-permute-start(bf16[3,64,2048]{2,1,0:T(8,128)(2,1)S(1)} %copy-done.19), channel_id=1, source_target_pairs={{0,2},{1,3},{2,0},{3,1},{4,6},{5,7},{6,4},{7,5},{8,10},{9,11},{10,... | collective-permute-start | bytes 2359304 | tf_op jit(solution)/shard_map/ppermute | solution.py:196
  74.2 36.5 %collective-permute-start.2 = (bf16[3,64,2048]{2,1,0:T(8,128)(2,1)S(1)}, bf16[3,64,2048]{2,1,0:T(8,128)(2,1)S(1)}, u32[]{:S(2)}, u32[]{:S(2)}) collective-permute-start(bf16[3,64,2048]{2,1,0:T(8,128)(2,1)S(1)} %copy-done.19), channel_id=1, source_target_pairs={{0,1},{1,2},{2,3},{3,0},{4,5},{5,6},{6,7},{7,4},{8,9},{9,10},{10,1... | collective-permute-start | bytes 2359304 | tf_op jit(solution)/shard_map/ppermute | solution.py:196
  110.7 1.9 copy-start.8
  116.3 1.3 copy-start.12
  121.0 1.4 copy-start.3
  122.4 72.1 %all-to-all-start.1 = ((bf16[32,2,64,256]{3,2,1,0:T(8,128)(2,1)}), bf16[32,2,64,256]{3,2,1,0:T(8,128)(2,1)}, u32[]{:S(2)}, u32[]{:S(2)}) async-start(bf16[32,2,64,256]{3,2,1,0:T(8,128)(2,1)} %bitcast.35), calls=%async_computation.1 | async-start | bytes 4194304 | tf_op jit(solution)/shard_map/all_to_all | solution.py:200
  128.9 26.1 %collective-permute-start.4 = (bf16[3,96,2048]{2,1,0:T(8,128)(2,1)}, bf16[3,96,2048]{2,1,0:T(8,128)(2,1)S(1)}, u32[]{:S(2)}, u32[]{:S(2)}) collective-permute-start(bf16[3,96,2048]{2,1,0:T(8,128)(2,1)} %copy-done.16), channel_id=1, source_target_pairs={{0,3},{1,0},{2,1},{3,2},{4,7},{5,4},{6,5},{7,6},{8,11},{9,8},{10,9... | collective-permute-start | bytes 3538952 | tf_op jit(solution)/shard_map/ppermute | solution.py:196
  129.6 27.0 %collective-permute-start.5 = (bf16[3,96,2048]{2,1,0:T(8,128)(2,1)}, bf16[3,96,2048]{2,1,0:T(8,128)(2,1)S(1)}, u32[]{:S(2)}, u32[]{:S(2)}) collective-permute-start(bf16[3,96,2048]{2,1,0:T(8,128)(2,1)} %copy-done.16), channel_id=1, source_target_pairs={{0,2},{1,3},{2,0},{3,1},{4,6},{5,7},{6,4},{7,5},{8,10},{9,11},{10,... | collective-permute-start | bytes 3538952 | tf_op jit(solution)/shard_map/ppermute | solution.py:196
  131.1 53.3 %collective-permute-start.6 = (bf16[3,96,2048]{2,1,0:T(8,128)(2,1)}, bf16[3,96,2048]{2,1,0:T(8,128)(2,1)S(1)}, u32[]{:S(2)}, u32[]{:S(2)}) collective-permute-start(bf16[3,96,2048]{2,1,0:T(8,128)(2,1)} %copy-done.16), channel_id=1, source_target_pairs={{0,1},{1,2},{2,3},{3,0},{4,5},{5,6},{6,7},{7,4},{8,9},{9,10},{10,1... | collective-permute-start | bytes 3538952 | tf_op jit(solution)/shard_map/ppermute | solution.py:196
  184.5 1.9 copy-start.9
  186.4 1.3 copy-start.17
  192.8 1.7 copy-start.11
  194.5 79.7 %all-to-all-start.2 = ((bf16[32,2,96,256]{3,2,1,0:T(8,128)(2,1)}), bf16[32,2,96,256]{3,2,1,0:T(8,128)(2,1)S(1)}, u32[]{:S(2)}, u32[]{:S(2)}) async-start(bf16[32,2,96,256]{3,2,1,0:T(8,128)(2,1)} %bitcast.34), calls=%async_computation.2 | async-start | bytes 6291456 | tf_op jit(solution)/shard_map/all_to_all | solution.py:200
  203.7 9.7 %collective-permute-start.12 = (bf16[3,32,2048]{2,1,0:T(8,128)(2,1)S(1)}, bf16[3,32,2048]{2,1,0:T(8,128)(2,1)S(1)}, u32[]{:S(2)}, u32[]{:S(2)}) collective-permute-start(bf16[3,32,2048]{2,1,0:T(8,128)(2,1)S(1)} %get-tuple-element.14.own_ref), channel_id=1, source_target_pairs={{0,3},{1,0},{2,1},{3,2},{4,7},{5,4},{6,5},{7,6},{8,11},{9,8},{10,9... | collective-permute-start | bytes 1179656 | tf_op jit(solution)/shard_map/ppermute | solution.py:196
  203.8 10.8 %collective-permute-start.13 = (bf16[3,32,2048]{2,1,0:T(8,128)(2,1)S(1)}, bf16[3,32,2048]{2,1,0:T(8,128)(2,1)S(1)}, u32[]{:S(2)}, u32[]{:S(2)}) collective-permute-start(bf16[3,32,2048]{2,1,0:T(8,128)(2,1)S(1)} %get-tuple-element.14.own_ref), channel_id=1, source_target_pairs={{0,2},{1,3},{2,0},{3,1},{4,6},{5,7},{6,4},{7,5},{8,10},{9,11},{10,... | collective-permute-start | bytes 1179656 | tf_op jit(solution)/shard_map/ppermute | solution.py:196
  205.2 19.6 %collective-permute-start.14 = (bf16[3,32,2048]{2,1,0:T(8,128)(2,1)S(1)}, bf16[3,32,2048]{2,1,0:T(8,128)(2,1)S(1)}, u32[]{:S(2)}, u32[]{:S(2)}) collective-permute-start(bf16[3,32,2048]{2,1,0:T(8,128)(2,1)S(1)} %get-tuple-element.14.own_ref), channel_id=1, source_target_pairs={{0,1},{1,2},{2,3},{3,0},{4,5},{5,6},{6,7},{7,4},{8,9},{9,10},{10,1... | collective-permute-start | bytes 1179656 | tf_op jit(solution)/shard_map/ppermute | solution.py:196
  224.8 1.9 copy-start.10
  229.2 1.0 copy-start.6
  274.1 11.8 %copy-start.1 = (bf16[32,2,96,256]{3,2,1,0:T(8,128)(2,1)}, bf16[32,2,96,256]{3,2,1,0:T(8,128)(2,1)S(1)}, u32[]{:S(2)}) copy-start(bf16[32,2,96,256]{3,2,1,0:T(8,128)(2,1)S(1)} %all-to-all-done.2.own_ref) | copy-start | bytes 9437188
  274.1 37.8 %all-to-all-start.4 = ((bf16[32,2,32,256]{3,2,1,0:T(8,128)(2,1)}), bf16[32,2,32,256]{3,2,1,0:T(8,128)(2,1)}, u32[]{:S(2)}, u32[]{:S(2)}) async-start(bf16[32,2,32,256]{3,2,1,0:T(8,128)(2,1)} %bitcast.33), calls=%async_computation.4 | async-start | bytes 2097152 | tf_op jit(solution)/shard_map/all_to_all | solution.py:200
  284.5 2.5 copy-start.4
  285.9 52.7 %collective-permute-start.7 = (bf16[32,96,256]{2,1,0:T(8,128)(2,1)}, bf16[32,96,256]{2,1,0:T(8,128)(2,1)}, u32[]{:S(2)}, u32[]{:S(2)}) collective-permute-start(bf16[32,96,256]{2,1,0:T(8,128)(2,1)} %slice_bitcast_fusion), channel_id=1, source_target_pairs={{0,4},{4,0},{1,5},{5,1},{2,6},{6,2},{3,7},{7,3},{8,12},{12,8},{9,1... | collective-permute-start | bytes 4718600 | tf_op jit(solution)/shard_map/ppermute | solution.py:196
  288.1 28.1 %copy-start.21 = (s32[1,12,3]{1,0,2:T(1,128)S(1)}, s32[1,12,3]{1,0,2:T(1,128)}, u32[]{:S(2)}) copy-start(s32[1,12,3]{1,0,2:T(1,128)} %param.10) | copy-start | bytes 436
  288.1 43.2 %copy-start = (bf16[1,16,256,256]{3,2,1,0:T(8,128)(2,1)S(1)}, bf16[1,16,256,256]{3,2,1,0:T(8,128)(2,1)}, u32[]{:S(2)}) copy-start(bf16[1,16,256,256]{3,2,1,0:T(8,128)(2,1)} %param.11) | copy-start | bytes 6291460
  288.1 46.4 %collective-permute-start.11 = (bf16[32,64,256]{2,1,0:T(8,128)(2,1)}, bf16[32,64,256]{2,1,0:T(8,128)(2,1)}, u32[]{:S(2)}, u32[]{:S(2)}) collective-permute-start(bf16[32,64,256]{2,1,0:T(8,128)(2,1)} %slice_bitcast_fusion.1), channel_id=1, source_target_pairs={{0,4},{4,0},{1,5},{5,1},{2,6},{6,2},{3,7},{7,3},{8,12},{12,8},{9,1... | collective-permute-start | bytes 3145736 | tf_op jit(solution)/shard_map/ppermute | solution.py:196
  291.2 52.3 %collective-permute-start.3 = (bf16[32,64,256]{2,1,0:T(8,128)(2,1)}, bf16[32,64,256]{2,1,0:T(8,128)(2,1)S(1)}, u32[]{:S(2)}, u32[]{:S(2)}) collective-permute-start(bf16[32,64,256]{2,1,0:T(8,128)(2,1)} %slice_bitcast_fusion.2), channel_id=1, source_target_pairs={{0,4},{4,0},{1,5},{5,1},{2,6},{6,2},{3,7},{7,3},{8,12},{12,8},{9,1... | collective-permute-start | bytes 3145736 | tf_op jit(solution)/shard_map/ppermute | solution.py:196
  313.8 17.5 %collective-permute-start.15 = (bf16[32,32,256]{2,1,0:T(8,128)(2,1)}, bf16[32,32,256]{2,1,0:T(8,128)(2,1)}, u32[]{:S(2)}, u32[]{:S(2)}) collective-permute-start(bf16[32,32,256]{2,1,0:T(8,128)(2,1)} %slice_bitcast_fusion.3), channel_id=1, source_target_pairs={{0,4},{4,0},{1,5},{5,1},{2,6},{6,2},{3,7},{7,3},{8,12},{12,8},{9,1... | collective-permute-start | bytes 1572872 | tf_op jit(solution)/shard_map/ppermute | solution.py:196
  331.3 3.2 copy-start.5
  334.5 4.1 %copy-start.2 = (bf16[32,2,96,256]{3,2,1,0:T(8,128)(2,1)S(1)}, bf16[32,2,96,256]{3,2,1,0:T(8,128)(2,1)}, u32[]{:S(2)}) copy-start(bf16[32,2,96,256]{3,2,1,0:T(8,128)(2,1)} %copy-done.1) | copy-start | bytes 9437188
